TPU v7x, 256 devices: a whole 4x4x8 slice. The times are simulated.
256 devices in a mesh: zero: 16 (over z, core), tp: 4 (over y), site: 4 (over x).
Axes of the slice: x: 4, y: 4, z: 8, core: 2. Of those that a mesh axis runs over, the one named last changes fastest.
Arguments:
- weight_gate: float32 [8192, 8192], P(('site', 'zero'), 'tp'), parts along dimension 0, may hold values from -0.1875 to 0.1875
- moment_gate: float32 [8192, 8192], P(('site', 'zero'), 'tp'), parts along dimension 0, may hold values from -0.125 to 0.125
- square_gate: float32 [8192, 8192], P(('site', 'zero'), 'tp'), parts along dimension 0, may hold values from -0.125 to 0.125
- weight_up: float32 [8192, 8192], P(('site', 'zero'), 'tp'), parts along dimension 0, may hold values from -0.1875 to 0.1875
- moment_up: float32 [8192, 8192], P(('site', 'zero'), 'tp'), parts along dimension 0, may hold values from -0.125 to 0.125
- square_up: float32 [8192, 8192], P(('site', 'zero'), 'tp'), parts along dimension 0, may hold values from -0.125 to 0.125
- norm_train: float32 [8192], P(('site', 'zero', 'tp')), parts along dimension 0, may hold values from 0.25 to 1.75
- norm_step: float32 [8192], P(('site', 'zero', 'tp')), parts along dimension 0, may hold values from -0.3 to 0.3
Outputs:
- ready_gate: bfloat16 [8192, 8192], P('site', 'tp'), parts along dimension 0
- ready_up: bfloat16 [8192, 8192], P('site', 'tp'), parts along dimension 0
- scale_gate: float32 [32768], P(('site', 'tp')), parts along dimension 0
- scale_up: float32 [32768], P(('site', 'tp')), parts along dimension 0
- serve_norm: bfloat16 [8192], P('site'), parts along dimension 0
- latest_gate: float32 [8192, 8192], P(('site', 'zero'), 'tp'), parts along dimension 0
- latest_up: float32 [8192, 8192], P(('site', 'zero'), 'tp'), parts along dimension 0
There are 4 independent parts, one for each index of `site`. A program takes and returns all parts, laid end to end along the dimension named above; each array names one. Nothing has to cross between parts.
All inputs are finite; a program needn't handle non-finite values. Where the computation divides by a largest or mean magnitude, that divisor is 1e-20 or more.
Results may differ from a plain program's by a relative error of at most 0.001.
Values may be sent and summed in bfloat16 or wider, within the bound.
No kernel may reach another device: no remote copies, remote signals or barrier semaphores. Data moves between devices by JAX's collectives and lax.ppermute only.
A program may use at most 128 MiB of HBM per device.

v0:
```python
import jax
import jax.numpy as jnp
from jax import lax
from jax.sharding import PartitionSpec as P

learn_rate = 0.25
hold_rate = 0.9


def from_everyone(array, axis):
    length = lax.axis_size(axis)
    return lax.all_to_all(
        jnp.broadcast_to(array[None], (length, *array.shape)), axis, 0, 0, tiled=True
    )


def taken_together(array, axis):
    everything = from_everyone(array, axis)
    return jnp.max(everything, axis=0)


def packed_total(arrays, axis):
    line, at, outs = (jnp.concatenate([a.reshape(-1) for a in arrays]), 0, [])
    total = taken_together(line, axis)
    for a in arrays:
        outs.append(total[at : at + a.size].reshape(a.shape))
        at += a.size
    return tuple(outs)


def sent_together(arrays, axis, dim, along):
    both = jnp.concatenate(arrays, axis=along)
    whole, at, outs = (lax.all_gather(both, axis, axis=dim, tiled=True), 0, [])
    for a in arrays:
        outs.append(lax.slice_in_dim(whole, at, at + a.shape[along], axis=along))
        at += a.shape[along]
    return tuple(outs)


def in_order(tiles, dim):
    shape = list(tiles.shape[1:])
    shape[dim] *= tiles.shape[0]
    return jnp.moveaxis(tiles, 0, dim).reshape(shape)


def gathered_copies(array, axis, dim):
    return in_order(from_everyone(array, axis), dim)


def per_device(
    weight_gate, moment_gate, square_gate, weight_up, moment_up, square_up, norm_train, norm_step
):
    hold_gate = hold_rate * moment_gate + square_gate
    latest_gate = weight_gate - learn_rate * hold_gate
    hold_up = hold_rate * moment_up + square_up
    latest_up = weight_up - learn_rate * hold_up
    scale_gate, scale_up = packed_total(
        (jnp.max(jnp.abs(latest_gate), axis=0), jnp.max(jnp.abs(latest_up), axis=0)), "zero"
    )
    narrow_gate, narrow_up = (
        (latest_gate / scale_gate).astype(jnp.bfloat16),
        (latest_up / scale_up).astype(jnp.bfloat16),
    )
    ready_gate, ready_up = sent_together((narrow_gate, narrow_up), "zero", 0, 1)
    serve_norm = gathered_copies((norm_train + norm_step).astype(jnp.bfloat16), ("zero", "tp"), 0)
    return (ready_gate, ready_up, scale_gate, scale_up, serve_norm, latest_gate, latest_up)


def solution(mesh):
    placed = (
        P(("site", "zero"), "tp"),
        P(("site", "zero"), "tp"),
        P(("site", "zero"), "tp"),
        P(("site", "zero"), "tp"),
        P(("site", "zero"), "tp"),
        P(("site", "zero"), "tp"),
        P(("site", "zero", "tp")),
        P(("site", "zero", "tp")),
    )
    return jax.shard_map(
        per_device,
        mesh=mesh,
        in_specs=placed,
        out_specs=(
            P("site", "tp"),
            P("site", "tp"),
            P(("site", "tp")),
            P(("site", "tp")),
            P("site"),
            P(("site", "zero"), "tp"),
            P(("site", "zero"), "tp"),
        ),
        check_vma=False,
    )
```

profile of v0, /device:TPU:1, one launch (start us, length us, event | category | flops | bytes accessed | tf_op | source)
XLA Modules:
  0.0 145.2 jit_solution(7938269426227200379)
XLA Ops:
  7.2 0.0 copy-start.4
  7.2 0.0 copy-start.5
  7.2 0.0 all-gather.2.cloned.1.call-start
  7.2 3.2 %abs_reduce_fusion = (f32[2048]{0:T(1024)S(1)}, f32[128,2048]{1,0:T(8,128)S(1)}, f32[2048]{0:T(1024)S(1)}, f32[128,2048]{1,0:T(8,128)S(1)}) fusion(f32[128,2048]{1,0:T(8,128)} %param.11, f32[128,2048]{1,0:T(8,128)} %param.13, f32[128,2048]{1,0:T(8,128)} %param.12, f32[128,2048]{1,0:T(8,128)} %param.8, f32[128,2048]{1,0:T(8,128)} %param.10, f32[128,2048]{1,0:T(8,128)} %param.9), kind=kLoop, calls=%fused_computation.3 | loop fusion | flops 3141632 | bytes 8404992 | tf_op jit(solution)/shard_map/reduce_max | solution.py:58
  10.5 0.0 copy-start
  10.5 0.0 copy-start.1
  10.5 0.2 broadcast_in_dim.4
  10.7 21.4 %all_to_all.12 = f32[16,1,4096]{2,1,0:T(1,128)S(1)} all-to-all(f32[16,1,4096]{2,1,0:T(1,128)S(1)} %broadcast_in_dim.4), channel_id=1, replica_groups=mesh['zero'=16,'tp'=4,'site'=4] {'zero'}, dimensions={0} | all-to-all | bytes 524288 | tf_op jit(solution)/shard_map/all_to_all | solution.py:12
  32.1 0.2 reduce_max.29
  32.2 0.0 copy-start.2
  32.3 0.0 copy-start.3
  32.3 0.1 divide_convert_fusion.1
  32.4 0.1 divide_convert_fusion
  32.5 1.1 pad_maximum_fusion
  33.5 0.0 all-gather.2.cloned.1.call-update
  33.5 0.0 copy-done.4
  33.6 0.0 copy-done.5
  33.6 15.2 %all_to_all.13 = bf16[64,1,32]{2,1,0:T(2,128)(2,1)S(1)} all-to-all(bf16[64,1,32]{2,1,0:T(2,128)(2,1)S(1)} %broadcast_in_dim.5), channel_id=1, replica_groups=mesh['zero'=16,'tp'=4,'site'=4] {'zero','tp'}, dimensions={0} | all-to-all | bytes 8192 | tf_op jit(solution)/shard_map/all_to_all | solution.py:12
  48.8 0.1 reduce.1
  48.9 0.7 reshape.32
  49.5 76.8 %all-gather.2.cloned.1.call-done = bf16[2048,4096]{1,0:T(8,128)(2,1)} async-done(((bf16[128,4096]{1,0:T(8,128)(2,1)}), bf16[2048,4096]{1,0:T(8,128)(2,1)}) %all-gather.2.cloned.1.call-update) | async-done | bytes 16777232 | tf_op jit(solution)/shard_map/all_gather | solution.py:33
  126.4 11.9 %fusion = (bf16[2048,2048]{1,0:T(8,128)(2,1)}, bf16[2048,2048]{1,0:T(8,128)(2,1)}) fusion(bf16[2048,4096]{1,0:T(8,128)(2,1)} %all-gather.2.cloned.1.call-done), kind=kLoop, calls=%fused_computation.9 | loop fusion | bytes 33554432 | tf_op jit(solution)/shard_map/slice | solution.py:35
  138.3 0.0 copy-done
  138.3 0.0 copy-done.1
  138.4 0.0 copy-done.2
  138.4 0.0 copy-done.3
  (4 shorter events, 0.0 us)
Async XLA Ops:
  7.2 26.4 %copy-start.4 = (f32[32]{0:T(128)S(1)}, f32[32]{0:T(128)}, u32[]{:S(2)}) copy-start(f32[32]{0:T(128)} %param.14) | copy-start | bytes 388
  7.2 26.4 %copy-start.5 = (f32[32]{0:T(128)S(1)}, f32[32]{0:T(128)}, u32[]{:S(2)}) copy-start(f32[32]{0:T(128)} %param.15) | copy-start | bytes 388
  7.2 119.2 %all-gather.2.cloned.1.call-start = ((), (), s32[]{:S(2)}) async-start(), calls=%async_computation.2 | async-start | bytes 17825792 | tf_op jit(solution)/shard_map/all_gather | solution.py:33
  10.5 127.9 %copy-start = (f32[128,2048]{1,0:T(8,128)}, f32[128,2048]{1,0:T(8,128)S(1)}, u32[]{:S(2)}) copy-start(f32[128,2048]{1,0:T(8,128)S(1)} %get-tuple-element.10) | copy-start | bytes 3145732
  10.5 127.9 %copy-start.1 = (f32[128,2048]{1,0:T(8,128)}, f32[128,2048]{1,0:T(8,128)S(1)}, u32[]{:S(2)}) copy-start(f32[128,2048]{1,0:T(8,128)S(1)} %get-tuple-element.16) | copy-start | bytes 3145732
  32.2 106.1 %copy-start.2 = (f32[2048]{0:T(1024)}, f32[2048]{0:T(1024)S(1)}, u32[]{:S(2)}) copy-start(f32[2048]{0:T(1024)S(1)} %get-tuple-element.13) | copy-start | bytes 24580
  32.3 106.1 %copy-start.3 = (f32[2048]{0:T(1024)}, f32[2048]{0:T(1024)S(1)}, u32[]{:S(2)}) copy-start(f32[2048]{0:T(1024)S(1)} %get-tuple-element.14) | copy-start | bytes 24580
Sparse Core Ops, SparseCore 0:
  33.7 92.6 all-gather.1
where the time goes:
time: 145 us
  waiting for transfers between devices  76.9 us (53%)
  blocking collectives  36.5 us (25%)
  between operations  14.2 us (10%)
  local copies, waits for them, and re-layouts  12.9 us (9%)
  other arithmetic  4.74 us (3%)
    all_gather x1, waiting for transfers between devices, sent_together(): whole, at, outs = (lax.all_gather(both, axis, axis=dim, tiled=True), 0, [])  76.8 us
    all_to_all x2, blocking collectives, from_everyone(): lax.all_to_all(jnp.broadcast_to(array[None], (length, *array.shape)), axi...  36.5 us
    slice x1, local copies, waits for them, and re-layouts, sent_together(): outs.append(lax.slice_in_dim(whole, at, at + a.shape[along], axis=along))  11.9 us
    reduce_max x1, other arithmetic, per_device(): jnp.max(jnp.abs(latest_up), axis=0)  3.23 us
  transfers between devices with their start and end apart: 1, of which 1 were waited for; matrix products, arithmetic and copies ran while one was open for 1% of the time, Pallas kernels for 0%

commit v1 on v0

v1 whole, which is shorter than its diff:
```python
import jax
import jax.numpy as jnp
from jax import lax
from jax.experimental import pallas as pl
from jax.experimental.pallas import tpu as pltpu
from jax.sharding import PartitionSpec as P


learn_rate = 0.25
hold_rate = 0.9

AXIS = "zero"
CORES = 2


def hop(array, step):
    n = lax.axis_size(AXIS) // CORES
    pairs = [(z * CORES + c, (z + step) % n * CORES + c) for z in range(n) for c in range(CORES)]
    return lax.ppermute(array, AXIS, pairs)


def swap(array):
    n = lax.axis_size(AXIS)
    return lax.ppermute(array, AXIS, [(i, i ^ 1) for i in range(n)])


def place(wholes, pieces):
    n = lax.axis_size(AXIS)
    depth = pieces[0][0].shape[0]
    fresh = isinstance(wholes[0], jax.ShapeDtypeStruct)

    def kernel(*refs):
        k = len(pieces)
        ins = refs[:k]
        outs = refs[-3:-1]
        sems = refs[-1]
        me = lax.axis_index(AXIS)
        chip, core = me // CORES, lax.rem(me, CORES)
        copies = []
        for i, (_, which, ahead, over) in enumerate(pieces):
            slot = lax.rem(chip + ahead, n // CORES) * CORES + lax.rem(core + over, CORES)
            rows = pl.ds(pl.multiple_of(slot * depth, depth), depth)
            copies.append(pltpu.make_async_copy(ins[i], outs[which].at[rows, :], sems.at[i]))
        for c in copies:
            c.start()
        for c in copies:
            c.wait()

    k = len(pieces)
    size = sum(p[0].size * 2 for p in pieces)
    anywhere = pl.BlockSpec(memory_space=pl.ANY)
    call = pl.pallas_call(
        kernel,
        out_shape=[jax.ShapeDtypeStruct(w.shape, w.dtype) for w in wholes],
        in_specs=[anywhere] * (k + (0 if fresh else 2)),
        out_specs=[anywhere] * 2,
        scratch_shapes=[pltpu.SemaphoreType.DMA((k,))],
        input_output_aliases={} if fresh else {k: 0, k + 1: 1},
        compiler_params=pltpu.CompilerParams(vmem_limit_bytes=1 << 20),
        cost_estimate=pl.CostEstimate(flops=size, bytes_accessed=2 * size, transcendentals=0),
    )
    args = [p[0] for p in pieces] + ([] if fresh else list(wholes))
    return call(*args)


def settle(wholes, brought):
    pieces = [(a, w, at, 0) for a, w, at in brought]
    pieces += [(swap(a), w, at, 1) for a, w, at in brought]
    return place(wholes, pieces)


def per_device(
    weight_gate, moment_gate, square_gate, weight_up, moment_up, square_up, norm_train, norm_step
):
    hold_gate = hold_rate * moment_gate + square_gate
    latest_gate = weight_gate - learn_rate * hold_gate
    hold_up = hold_rate * moment_up + square_up
    latest_up = weight_up - learn_rate * hold_up
    width = latest_gate.shape[1]
    members = lax.axis_size(AXIS)
    chips = members // CORES
    half = chips // 2

    gain = (norm_train + norm_step).astype(jnp.bfloat16).astype(jnp.float32)
    own = jnp.concatenate(
        [
            jnp.max(jnp.abs(latest_gate), axis=0),
            jnp.max(jnp.abs(latest_up), axis=0),
            jnp.pad(gain, (0, 1024 - gain.shape[0])),
        ]
    )
    notes = {0: own}
    ahead = back = own
    for d in range(1, half + 1):
        back = hop(back, 1)
        notes[chips - d] = back
        if d < half:
            ahead = hop(ahead, -1)
            notes[d] = ahead
    mine = jnp.stack([notes[k] for k in range(chips)])
    theirs = swap(mine)
    top = jnp.max(jnp.maximum(mine, theirs), axis=0)
    scale_gate = top[:width]
    scale_up = top[width : 2 * width]

    narrow_gate = (latest_gate / scale_gate).astype(jnp.bfloat16)
    narrow_up = (latest_up / scale_up).astype(jnp.bfloat16)

    wholes = [jax.ShapeDtypeStruct((members * a.shape[0], width), a.dtype) for a in (narrow_gate, narrow_up)]
    held = {-1: [(narrow_gate, 0, 0), (narrow_up, 1, 0)], 0: [(narrow_up, 1, 0), (narrow_gate, 0, 0)]}
    steps = 2 * half - 1
    for k in range(1, steps + 1):
        d = (k + 1) // 2
        if k >= 3:
            sent = [a for a, _, _ in held[k - 2]]
            sent, wholes = lax.optimization_barrier((sent, list(wholes)))
            held[k - 2] = [(s, w, at) for s, (_, w, at) in zip(sent, held[k - 2])]
        (a, wa, _), (b, wb, _) = held[k - 2]
        held[k] = [(hop(a, 1), wa, chips - d), (hop(b, -1), wb, d)]
        if k != 1 and k != 2:
            wholes = settle(wholes, held[k - 2])
        elif k == 2:
            wholes = settle(wholes, held[-1])
    brought, wholes = lax.optimization_barrier(([a for a, _, _ in held[steps]], list(wholes)))
    held[steps] = [(b, w, at) for b, (_, w, at) in zip(brought, held[steps])]
    for k in (steps - 1, steps):
        wholes = settle(wholes, held[k])

    chip, core = lax.axis_index(AXIS) // CORES, lax.axis_index(AXIS) % CORES
    many = norm_train.shape[0]
    gains = [a[:, 2 * width : 2 * width + many] for a in (mine, theirs)]
    low, high = jnp.where(core == 0, gains[0], gains[1]), jnp.where(core == 0, gains[1], gains[0])
    line = jnp.concatenate([low, high], axis=1)
    line = lax.dynamic_slice_in_dim(jnp.concatenate([line, line]), (chips - chip) % chips, chips, axis=0)
    line = line.reshape(members, many)
    t = lax.axis_size("tp")
    parts = [line]
    for d in range(1, t):
        parts.append(lax.ppermute(line, "tp", [((i + d) % t, i) for i in range(t)]))
    both = jnp.concatenate(parts + parts, axis=1)
    at = (t - lax.axis_index("tp")) % t
    line = lax.dynamic_slice_in_dim(both, at * many, t * many, axis=1)
    serve_norm = line.reshape(-1).astype(jnp.bfloat16)
    return (wholes[0], wholes[1], scale_gate, scale_up, serve_norm, latest_gate, latest_up)


def solution(mesh):
    return shard(mesh, per_device)


def shard(mesh, step):
    placed = (P(("site", "zero"), "tp"),) * 6 + (P(("site", "zero", "tp")),) * 2
    return jax.shard_map(
        step,
        mesh=mesh,
        in_specs=placed,
        out_specs=(
            P("site", "tp"),
            P("site", "tp"),
            P(("site", "tp")),
            P(("site", "tp")),
            P("site"),
            P(("site", "zero"), "tp"),
            P(("site", "zero"), "tp"),
        ),
        check_vma=False,
    )
```

time: 145 us -> 183 us (1.26); the launches traced: 145 us -> 181 us
  starting transfers between devices: 0.04 us -> 53.5 us
  Pallas kernels: 0 us -> 42.3 us
  blocking collectives: 36.5 us -> 0 us
  between operations: 14.2 us -> 1.03 us
  local copies, waits for them, and re-layouts: 12.9 us -> 1.12 us
  waiting for transfers between devices: 76.9 us -> 78.9 us
    ppermute x0 -> x41, waiting for transfers between devices: none -> 78.9 us  [the longest x21 71.1 us: hop(): return lax.ppermute(array, AXIS, pairs)]
    all_gather x1 -> x0, waiting for transfers between devices: 76.8 us -> none  [sent_together(): whole, at, outs = (lax.all_gather(both, axis, axis=dim, tiled=True), 0, [])]
    ppermute x0 -> x41, starting transfers between devices: none -> 53.5 us  [the longest x21 28.4 us: hop(): return lax.ppermute(array, AXIS, pairs)]
    pallas_call x0 -> x8, Pallas kernels: none -> 42.3 us  [place(): return call(*args)]
    all_to_all x2 -> x0, blocking collectives: 36.5 us -> none  [from_everyone(): lax.all_to_all(jnp.broadcast_to(array[None], (length, *array.shape)), axi...]
    slice x2 -> x1, local copies, waits for them, and re-layouts: 12 us -> 0.01 us  [per_device(): scale_up = top[width:2 * width]]
  transfers between devices with their start and end apart: 1 -> 41, of which waited for: 1 -> 18; matrix products, arithmetic and copies ran while one was open for 1% -> 1% of each run, Pallas kernels for 0% -> 5%
where the time goes in v1:
time: 183 us; the launch traced here: 181 us
  waiting for transfers between devices  78.9 us (43%)
  starting transfers between devices  53.5 us (29%)
  Pallas kernels  42.3 us (23%)
  other arithmetic  4.23 us (2%)
    ppermute x21, waiting for transfers between devices, hop(): return lax.ppermute(array, AXIS, pairs)  71.1 us
    pallas_call x8, Pallas kernels, place(): return call(*args)  42.3 us
    ppermute x21, starting transfers between devices, hop(): return lax.ppermute(array, AXIS, pairs)  28.4 us
    ppermute x17, starting transfers between devices, swap(): return lax.ppermute(array, AXIS, [(i, i ^ 1) for i in range(n)])  20 us
    ppermute x3, waiting for transfers between devices, per_device(): parts.append(lax.ppermute(line, 'tp', [((i + d) % t, i) for i in range(t)]))  6.22 us
    ppermute x3, starting transfers between devices, per_device(): parts.append(lax.ppermute(line, 'tp', [((i + d) % t, i) for i in range(t)]))  5.14 us
  transfers between devices with their start and end apart: 41, of which 18 were waited for; matrix products, arithmetic and copies ran while one was open for 1% of the time, Pallas kernels for 5%

profile of v1, /device:TPU:1, one launch (start us, length us, event | category | flops | bytes accessed | tf_op | source)
XLA Modules:
  0.0 181.1 jit_solution(663475631104351138)
XLA Ops:
  0.6 0.7 add_convert_fusion
  1.3 3.2 %abs_reduce_fusion = (f32[2048]{0:T(1024)S(1)}, f32[128,2048]{1,0:T(8,128)S(1)}, f32[2048]{0:T(1024)S(1)}, f32[128,2048]{1,0:T(8,128)S(1)}) fusion(f32[128,2048]{1,0:T(8,128)} %param.11, f32[128,2048]{1,0:T(8,128)} %param.13, f32[128,2048]{1,0:T(8,128)} %param.12, f32[128,2048]{1,0:T(8,128)} %param.8, f32[128,2048]{1,0:T(8,128)} %param.10, f32[128,2048]{1,0:T(8,128)} %param.9), kind=kLoop, calls=%fused_computation.2 | loop fusion | flops 3141632 | bytes 8404992 | tf_op jit(solution)/shard_map/reduce_max | solution.py:88
  4.6 2.5 %collective-permute-start.3 = (f32[5120]{0:T(1024)S(1)}, f32[5120]{0:T(1024)S(1)}, u32[]{:S(2)}, u32[]{:S(2)}) collective-permute-start(f32[5120]{0:T(1024)S(1)} %pad_maximum_fusion), channel_id=1, source_target_pairs={{0,32},{16,48},{32,64},{48,80},{64,96},{80,112},{96,128},{112,144}... | collective-permute-start | bytes 61448 | tf_op jit(solution)/shard_map/ppermute | solution.py:19
  7.1 4.0 %collective-permute-start = (f32[5120]{0:T(1024)S(1)}, f32[5120]{0:T(1024)S(1)}, u32[]{:S(2)}, u32[]{:S(2)}) collective-permute-start(f32[5120]{0:T(1024)S(1)} %pad_maximum_fusion), channel_id=1, source_target_pairs={{0,224},{16,240},{32,0},{48,16},{64,32},{80,48},{96,64},{112,80},{... | collective-permute-start | bytes 61448 | tf_op jit(solution)/shard_map/ppermute | solution.py:19
  11.1 1.1 collective-permute-done.3
  12.2 2.8 %collective-permute-start.1 = (f32[5120]{0:T(1024)S(1)}, f32[5120]{0:T(1024)S(1)}, u32[]{:S(2)}, u32[]{:S(2)}) collective-permute-start(f32[5120]{0:T(1024)S(1)} %collective-permute-done), channel_id=1, source_target_pairs={{0,224},{16,240},{32,0},{48,16},{64,32},{80,48},{96,64},{112,80},{... | collective-permute-start | bytes 61448 | tf_op jit(solution)/shard_map/ppermute | solution.py:19
  15.0 1.1 collective-permute-done.4
  16.1 2.8 %collective-permute-start.2 = (f32[5120]{0:T(1024)S(1)}, f32[5120]{0:T(1024)S(1)}, u32[]{:S(2)}, u32[]{:S(2)}) collective-permute-start(f32[5120]{0:T(1024)S(1)} %collective-permute-done.1), channel_id=1, source_target_pairs={{0,224},{16,240},{32,0},{48,16},{64,32},{80,48},{96,64},{112,80},{... | collective-permute-start | bytes 61448 | tf_op jit(solution)/shard_map/ppermute | solution.py:19
  18.8 1.1 collective-permute-done.5
  19.9 3.8 %collective-permute-done.6 = f32[5120]{0:T(1024)S(1)} collective-permute-done((f32[5120]{0:T(1024)S(1)}, f32[5120]{0:T(1024)S(1)}, u32[]{:S(2)}, u32[]{:S(2)}) %collective-permute-start.6) | collective-permute-done | bytes 20512 | tf_op jit(solution)/shard_map/ppermute | solution.py:19
  23.8 0.2 stack.35
  24.0 5.1 %collective-permute-start.7 = (f32[8,5120]{1,0:T(8,128)S(1)}, f32[8,5120]{1,0:T(8,128)S(1)}, u32[]{:S(2)}, u32[]{:S(2)}) collective-permute-start(f32[8,5120]{1,0:T(8,128)S(1)} %stack.35), channel_id=1, source_target_pairs={{0,16},{16,0},{32,48},{48,32},{64,80},{80,64},{96,112},{112,96},{1... | collective-permute-start | bytes 491528 | tf_op jit(solution)/shard_map/ppermute | solution.py:24
  29.1 1.0 collective-permute-done.7
  30.2 0.1 divide_convert_fusion.refs_1_
  30.3 0.5 collective-permute-start.11
  30.8 0.1 divide_convert_fusion.1.refs_0_
  30.8 0.2 collective-permute-start.10
  31.1 1.5 collective-permute-start.8
  32.5 0.5 collective-permute-done.10.refs_2_
  33.0 1.3 shard_map.135
  34.4 9.8 %collective-permute-done.9.refs_1_ = bf16[128,2048]{1,0:T(8,128)(2,1)S(1)} collective-permute-done((bf16[128,2048]{1,0:T(8,128)(2,1)S(1)}, bf16[128,2048]{1,0:T(8,128)(2,1)S(1)}, u32[]{:S(2)}, u32[]{:S(2)}) %collective-permute-start.9) | collective-permute-done | bytes 524320 | tf_op jit(solution)/shard_map/ppermute | solution.py:19
  44.2 1.3 collective-permute-done.8.refs_0_
  45.5 1.2 collective-permute-start.16
  46.7 0.2 collective-permute-start.14
  46.9 2.5 %collective-permute-start.15 = (bf16[128,2048]{1,0:T(8,128)(2,1)S(1)}, bf16[128,2048]{1,0:T(8,128)(2,1)S(1)}, u32[]{:S(2)}, u32[]{:S(2)}) collective-permute-start(bf16[128,2048]{1,0:T(8,128)(2,1)S(1)} %divide_convert_fusion.1.refs_0_), channel_id=1, source_target_pairs={{0,224},{16,240},{32,0},{48,16},{64,32},{80,48},{96,64},{112,80},{... | collective-permute-start | bytes 1572872 | tf_op jit(solution)/shard_map/ppermute | solution.py:19
  49.4 1.3 shard_map.136
  50.7 10.1 %collective-permute-done.14.refs_0_ = bf16[128,2048]{1,0:T(8,128)(2,1)S(1)} collective-permute-done((bf16[128,2048]{1,0:T(8,128)(2,1)S(1)}, bf16[128,2048]{1,0:T(8,128)(2,1)S(1)}, u32[]{:S(2)}, u32[]{:S(2)}) %collective-permute-start.14) | collective-permute-done | bytes 524320 | tf_op jit(solution)/shard_map/ppermute | solution.py:19
  60.9 1.4 collective-permute-start.18
  62.2 2.7 %collective-permute-start.13 = (bf16[128,2048]{1,0:T(8,128)(2,1)S(1)}, bf16[128,2048]{1,0:T(8,128)(2,1)S(1)}, u32[]{:S(2)}, u32[]{:S(2)}) collective-permute-start(bf16[128,2048]{1,0:T(8,128)(2,1)S(1)} %collective-permute-done.9.refs_1_), channel_id=1, source_target_pairs={{0,224},{16,240},{32,0},{48,16},{64,32},{80,48},{96,64},{112,80},{... | collective-permute-start | bytes 1572872 | tf_op jit(solution)/shard_map/ppermute | solution.py:19
  64.9 1.3 shard_map.137
  66.3 10.1 %collective-permute-done.12.refs_0_ = bf16[128,2048]{1,0:T(8,128)(2,1)S(1)} collective-permute-done((bf16[128,2048]{1,0:T(8,128)(2,1)S(1)}, bf16[128,2048]{1,0:T(8,128)(2,1)S(1)}, u32[]{:S(2)}, u32[]{:S(2)}) %collective-permute-start.12) | collective-permute-done | bytes 524320 | tf_op jit(solution)/shard_map/ppermute | solution.py:19
  76.4 1.4 collective-permute-start.24
  77.8 2.5 %collective-permute-start.22 = (bf16[128,2048]{1,0:T(8,128)(2,1)S(1)}, bf16[128,2048]{1,0:T(8,128)(2,1)S(1)}, u32[]{:S(2)}, u32[]{:S(2)}) collective-permute-start(bf16[128,2048]{1,0:T(8,128)(2,1)S(1)} %collective-permute-done.14.refs_0_), channel_id=1, source_target_pairs={{0,32},{16,48},{32,64},{48,80},{64,96},{80,112},{96,128},{112,144}... | collective-permute-start | bytes 1572872 | tf_op jit(solution)/shard_map/ppermute | solution.py:19
  80.2 0.2 collective-permute-start.23
  80.5 1.3 shard_map.138
  81.8 10.1 %collective-permute-done.22.refs_0_ = bf16[128,2048]{1,0:T(8,128)(2,1)S(1)} collective-permute-done((bf16[128,2048]{1,0:T(8,128)(2,1)S(1)}, bf16[128,2048]{1,0:T(8,128)(2,1)S(1)}, u32[]{:S(2)}, u32[]{:S(2)}) %collective-permute-start.22) | collective-permute-done | bytes 524320 | tf_op jit(solution)/shard_map/ppermute | solution.py:19
  92.0 1.0 collective-permute-done.23.refs_1_
  92.9 1.6 collective-permute-start.26
  94.6 1.5 collective-permute-start.20
  96.1 1.2 collective-permute-start.21
  97.3 0.3 collective-permute-start.34
  97.5 2.4 %collective-permute-start.35 = (bf16[128,2048]{1,0:T(8,128)(2,1)S(1)}, bf16[128,2048]{1,0:T(8,128)(2,1)S(1)}, u32[]{:S(2)}, u32[]{:S(2)}) collective-permute-start(bf16[128,2048]{1,0:T(8,128)(2,1)S(1)} %collective-permute-done.23.refs_1_), channel_id=1, source_target_pairs={{0,224},{16,240},{32,0},{48,16},{64,32},{80,48},{96,64},{112,80},{... | collective-permute-start | bytes 1572872 | tf_op jit(solution)/shard_map/ppermute | solution.py:19
  100.0 1.3 shard_map.139
  101.3 7.5 %collective-permute-done.20.refs_0_ = bf16[128,2048]{1,0:T(8,128)(2,1)S(1)} collective-permute-done((bf16[128,2048]{1,0:T(8,128)(2,1)S(1)}, bf16[128,2048]{1,0:T(8,128)(2,1)S(1)}, u32[]{:S(2)}, u32[]{:S(2)}) %collective-permute-start.20) | collective-permute-done | bytes 524320 | tf_op jit(solution)/shard_map/ppermute | solution.py:19
  108.8 2.9 %collective-permute-start.30 = (bf16[128,2048]{1,0:T(8,128)(2,1)S(1)}, bf16[128,2048]{1,0:T(8,128)(2,1)S(1)}, u32[]{:S(2)}, u32[]{:S(2)}) collective-permute-start(bf16[128,2048]{1,0:T(8,128)(2,1)S(1)} %collective-permute-done.20.refs_0_), channel_id=1, source_target_pairs={{0,16},{16,0},{32,48},{48,32},{64,80},{80,64},{96,112},{112,96},{1... | collective-permute-start | bytes 1572872 | tf_op jit(solution)/shard_map/ppermute | solution.py:24
  111.6 1.2 collective-permute-start.28
  112.9 7.2 %collective-permute-done.34.refs_0_ = bf16[128,2048]{1,0:T(8,128)(2,1)S(1)} collective-permute-done((bf16[128,2048]{1,0:T(8,128)(2,1)S(1)}, bf16[128,2048]{1,0:T(8,128)(2,1)S(1)}, u32[]{:S(2)}, u32[]{:S(2)}) %collective-permute-start.34) | collective-permute-done | bytes 524320 | tf_op jit(solution)/shard_map/ppermute | solution.py:19
  120.0 0.2 collective-permute-start.29
  120.2 2.6 %collective-permute-start.36 = (bf16[128,2048]{1,0:T(8,128)(2,1)S(1)}, bf16[128,2048]{1,0:T(8,128)(2,1)S(1)}, u32[]{:S(2)}, u32[]{:S(2)}) collective-permute-start(bf16[128,2048]{1,0:T(8,128)(2,1)S(1)} %collective-permute-done.34.refs_0_), channel_id=1, source_target_pairs={{0,16},{16,0},{32,48},{48,32},{64,80},{80,64},{96,112},{112,96},{1... | collective-permute-start | bytes 1572872 | tf_op jit(solution)/shard_map/ppermute | solution.py:24
  122.8 0.1 collective-permute-start.37
  122.9 1.3 shard_map.140
  124.3 6.9 %collective-permute-done.28.refs_0_ = bf16[128,2048]{1,0:T(8,128)(2,1)S(1)} collective-permute-done((bf16[128,2048]{1,0:T(8,128)(2,1)S(1)}, bf16[128,2048]{1,0:T(8,128)(2,1)S(1)}, u32[]{:S(2)}, u32[]{:S(2)}) %collective-permute-start.28) | collective-permute-done | bytes 524320 | tf_op jit(solution)/shard_map/ppermute | solution.py:19
  131.2 3.1 %collective-permute-start.32 = (bf16[128,2048]{1,0:T(8,128)(2,1)S(1)}, bf16[128,2048]{1,0:T(8,128)(2,1)}, u32[]{:S(2)}, u32[]{:S(2)}) collective-permute-start(bf16[128,2048]{1,0:T(8,128)(2,1)S(1)} %collective-permute-done.28.refs_0_), channel_id=1, source_target_pairs={{0,16},{16,0},{32,48},{48,32},{64,80},{80,64},{96,112},{112,96},{1... | collective-permute-start | bytes 1572872 | tf_op jit(solution)/shard_map/ppermute | solution.py:24
  134.4 0.1 fusion.2
  134.5 2.7 %collective-permute-start.38 = (bf16[16,32]{1,0:T(8,128)(2,1)S(1)}, bf16[16,32]{1,0:T(8,128)(2,1)S(1)}, u32[]{:S(2)}, u32[]{:S(2)}) collective-permute-start(bf16[16,32]{1,0:T(8,128)(2,1)S(1)} %reshape.21), channel_id=1, source_target_pairs={{4,0},{8,4},{12,8},{0,12},{5,1},{9,5},{13,9},{1,13},{6,2},{10,6},{... | collective-permute-start | bytes 3080 | tf_op jit(solution)/shard_map/ppermute | solution.py:139
  137.3 0.8 collective-permute-done.38
  138.0 1.9 %collective-permute-start.39 = (bf16[16,32]{1,0:T(8,128)(2,1)S(1)}, bf16[16,32]{1,0:T(8,128)(2,1)S(1)}, u32[]{:S(2)}, u32[]{:S(2)}) collective-permute-start(bf16[16,32]{1,0:T(8,128)(2,1)S(1)} %reshape.21), channel_id=1, source_target_pairs={{8,0},{12,4},{0,8},{4,12},{9,1},{13,5},{1,9},{5,13},{10,2},{14,6},... | collective-permute-start | bytes 3080 | tf_op jit(solution)/shard_map/ppermute | solution.py:139
  139.9 2.1 %collective-permute-done.39 = bf16[16,32]{1,0:T(8,128)(2,1)S(1)} collective-permute-done((bf16[16,32]{1,0:T(8,128)(2,1)S(1)}, bf16[16,32]{1,0:T(8,128)(2,1)S(1)}, u32[]{:S(2)}, u32[]{:S(2)}) %collective-permute-start.39) | collective-permute-done | bytes 1056 | tf_op jit(solution)/shard_map/ppermute | solution.py:139
  142.0 0.5 collective-permute-start.40
  142.5 3.4 %collective-permute-done.40 = bf16[16,32]{1,0:T(8,128)(2,1)S(1)} collective-permute-done((bf16[16,32]{1,0:T(8,128)(2,1)S(1)}, bf16[16,32]{1,0:T(8,128)(2,1)S(1)}, u32[]{:S(2)}, u32[]{:S(2)}) %collective-permute-start.40) | collective-permute-done | bytes 1056 | tf_op jit(solution)/shard_map/ppermute | solution.py:139
  145.9 0.1 concatenate.15
  146.0 0.7 fusion
  146.7 1.3 shard_map.141
  148.0 32.9 %shard_map.142 = (bf16[2048,2048]{1,0:T(8,128)(2,1)}, bf16[2048,2048]{1,0:T(8,128)(2,1)}) custom-call(bf16[128,2048]{1,0:T(8,128)(2,1)S(1)} %collective-permute-done.28.refs_0_, bf16[128,2048]{1,0:T(8,128)(2,1)S(1)} %collective-permute-done.29.refs_1_, ...), custom_call_target="tpu_custom_call", output_to_operand_aliasing={{0}: (4, {}), {1}: (5, {})} | custom-call | flops 2097152 | bytes 4194304 | tf_op jit(solution)/shard_map/pallas_call | solution.py:63
  (48 shorter events, 0.3 us)
Async XLA Ops:
  4.5 46.2 %copy-start = (f32[128,2048]{1,0:T(8,128)}, f32[128,2048]{1,0:T(8,128)S(1)}, u32[]{:S(2)}) copy-start(f32[128,2048]{1,0:T(8,128)S(1)} %get-tuple-element.90) | copy-start | bytes 3145732
  4.6 46.2 %copy-start.1 = (f32[128,2048]{1,0:T(8,128)}, f32[128,2048]{1,0:T(8,128)S(1)}, u32[]{:S(2)}) copy-start(f32[128,2048]{1,0:T(8,128)S(1)} %get-tuple-element.96) | copy-start | bytes 3145732
  4.6 7.6 %collective-permute-start.3 = (f32[5120]{0:T(1024)S(1)}, f32[5120]{0:T(1024)S(1)}, u32[]{:S(2)}, u32[]{:S(2)}) collective-permute-start(f32[5120]{0:T(1024)S(1)} %pad_maximum_fusion), channel_id=1, source_target_pairs={{0,32},{16,48},{32,64},{48,80},{64,96},{80,112},{96,128},{112,144}... | collective-permute-start | bytes 61448 | tf_op jit(solution)/shard_map/ppermute | solution.py:19
  7.1 5.1 %collective-permute-start = (f32[5120]{0:T(1024)S(1)}, f32[5120]{0:T(1024)S(1)}, u32[]{:S(2)}, u32[]{:S(2)}) collective-permute-start(f32[5120]{0:T(1024)S(1)} %pad_maximum_fusion), channel_id=1, source_target_pairs={{0,224},{16,240},{32,0},{48,16},{64,32},{80,48},{96,64},{112,80},{... | collective-permute-start | bytes 61448 | tf_op jit(solution)/shard_map/ppermute | solution.py:19
  12.2 3.8 %collective-permute-start.4 = (f32[5120]{0:T(1024)S(1)}, f32[5120]{0:T(1024)S(1)}, u32[]{:S(2)}, u32[]{:S(2)}) collective-permute-start(f32[5120]{0:T(1024)S(1)} %collective-permute-done.3), channel_id=1, source_target_pairs={{0,32},{16,48},{32,64},{48,80},{64,96},{80,112},{96,128},{112,144}... | collective-permute-start | bytes 61448 | tf_op jit(solution)/shard_map/ppermute | solution.py:19
  12.2 3.8 %collective-permute-start.1 = (f32[5120]{0:T(1024)S(1)}, f32[5120]{0:T(1024)S(1)}, u32[]{:S(2)}, u32[]{:S(2)}) collective-permute-start(f32[5120]{0:T(1024)S(1)} %collective-permute-done), channel_id=1, source_target_pairs={{0,224},{16,240},{32,0},{48,16},{64,32},{80,48},{96,64},{112,80},{... | collective-permute-start | bytes 61448 | tf_op jit(solution)/shard_map/ppermute | solution.py:19
  16.1 3.8 %collective-permute-start.5 = (f32[5120]{0:T(1024)S(1)}, f32[5120]{0:T(1024)S(1)}, u32[]{:S(2)}, u32[]{:S(2)}) collective-permute-start(f32[5120]{0:T(1024)S(1)} %collective-permute-done.4), channel_id=1, source_target_pairs={{0,32},{16,48},{32,64},{48,80},{64,96},{80,112},{96,128},{112,144}... | collective-permute-start | bytes 61448 | tf_op jit(solution)/shard_map/ppermute | solution.py:19
  16.1 3.8 %collective-permute-start.2 = (f32[5120]{0:T(1024)S(1)}, f32[5120]{0:T(1024)S(1)}, u32[]{:S(2)}, u32[]{:S(2)}) collective-permute-start(f32[5120]{0:T(1024)S(1)} %collective-permute-done.1), channel_id=1, source_target_pairs={{0,224},{16,240},{32,0},{48,16},{64,32},{80,48},{96,64},{112,80},{... | collective-permute-start | bytes 61448 | tf_op jit(solution)/shard_map/ppermute | solution.py:19
  19.9 3.8 %collective-permute-start.6 = (f32[5120]{0:T(1024)S(1)}, f32[5120]{0:T(1024)S(1)}, u32[]{:S(2)}, u32[]{:S(2)}) collective-permute-start(f32[5120]{0:T(1024)S(1)} %collective-permute-done.5), channel_id=1, source_target_pairs={{0,32},{16,48},{32,64},{48,80},{64,96},{80,112},{96,128},{112,144}... | collective-permute-start | bytes 61448 | tf_op jit(solution)/shard_map/ppermute | solution.py:19
  24.0 6.1 %collective-permute-start.7 = (f32[8,5120]{1,0:T(8,128)S(1)}, f32[8,5120]{1,0:T(8,128)S(1)}, u32[]{:S(2)}, u32[]{:S(2)}) collective-permute-start(f32[8,5120]{1,0:T(8,128)S(1)} %stack.35), channel_id=1, source_target_pairs={{0,16},{16,0},{32,48},{48,32},{64,80},{80,64},{96,112},{112,96},{1... | collective-permute-start | bytes 491528 | tf_op jit(solution)/shard_map/ppermute | solution.py:24
  30.2 20.6 %copy-start.2 = (f32[2048]{0:T(1024)}, f32[2048]{0:T(1024)S(1)}, u32[]{:S(2)}) copy-start(f32[2048]{0:T(1024)S(1)} %get-tuple-element.93) | copy-start | bytes 24580
  30.2 20.6 %copy-start.3 = (f32[2048]{0:T(1024)}, f32[2048]{0:T(1024)S(1)}, u32[]{:S(2)}) copy-start(f32[2048]{0:T(1024)S(1)} %get-tuple-element.94) | copy-start | bytes 24580
  30.3 2.3 %collective-permute-start.11 = (bf16[128,2048]{1,0:T(8,128)(2,1)S(1)}, bf16[128,2048]{1,0:T(8,128)(2,1)S(1)}, u32[]{:S(2)}, u32[]{:S(2)}) collective-permute-start(bf16[128,2048]{1,0:T(8,128)(2,1)S(1)} %divide_convert_fusion.refs_1_), channel_id=1, source_target_pairs={{0,16},{16,0},{32,48},{48,32},{64,80},{80,64},{96,112},{112,96},{1... | collective-permute-start | bytes 1572872 | tf_op jit(solution)/shard_map/ppermute | solution.py:24
  30.8 2.2 %collective-permute-start.10 = (bf16[128,2048]{1,0:T(8,128)(2,1)S(1)}, bf16[128,2048]{1,0:T(8,128)(2,1)S(1)}, u32[]{:S(2)}, u32[]{:S(2)}) collective-permute-start(bf16[128,2048]{1,0:T(8,128)(2,1)S(1)} %divide_convert_fusion.1.refs_0_), channel_id=1, source_target_pairs={{0,16},{16,0},{32,48},{48,32},{64,80},{80,64},{96,112},{112,96},{1... | collective-permute-start | bytes 1572872 | tf_op jit(solution)/shard_map/ppermute | solution.py:24
  31.1 13.1 %collective-permute-start.9 = (bf16[128,2048]{1,0:T(8,128)(2,1)S(1)}, bf16[128,2048]{1,0:T(8,128)(2,1)S(1)}, u32[]{:S(2)}, u32[]{:S(2)}) collective-permute-start(bf16[128,2048]{1,0:T(8,128)(2,1)S(1)} %divide_convert_fusion.refs_1_), channel_id=1, source_target_pairs={{0,224},{16,240},{32,0},{48,16},{64,32},{80,48},{96,64},{112,80},{... | collective-permute-start | bytes 1572872 | tf_op jit(solution)/shard_map/ppermute | solution.py:19
  31.1 14.4 %collective-permute-start.8 = (bf16[128,2048]{1,0:T(8,128)(2,1)S(1)}, bf16[128,2048]{1,0:T(8,128)(2,1)S(1)}, u32[]{:S(2)}, u32[]{:S(2)}) collective-permute-start(bf16[128,2048]{1,0:T(8,128)(2,1)S(1)} %divide_convert_fusion.1.refs_0_), channel_id=1, source_target_pairs={{0,32},{16,48},{32,64},{48,80},{64,96},{80,112},{96,128},{112,144}... | collective-permute-start | bytes 1572872 | tf_op jit(solution)/shard_map/ppermute | solution.py:19
  45.5 3.9 %collective-permute-start.16 = (bf16[128,2048]{1,0:T(8,128)(2,1)S(1)}, bf16[128,2048]{1,0:T(8,128)(2,1)S(1)}, u32[]{:S(2)}, u32[]{:S(2)}) collective-permute-start(bf16[128,2048]{1,0:T(8,128)(2,1)S(1)} %collective-permute-done.8.refs_0_), channel_id=1, source_target_pairs={{0,16},{16,0},{32,48},{48,32},{64,80},{80,64},{96,112},{112,96},{1... | collective-permute-start | bytes 1572872 | tf_op jit(solution)/shard_map/ppermute | solution.py:24
  46.7 2.7 %collective-permute-start.17 = (bf16[128,2048]{1,0:T(8,128)(2,1)S(1)}, bf16[128,2048]{1,0:T(8,128)(2,1)S(1)}, u32[]{:S(2)}, u32[]{:S(2)}) collective-permute-start(bf16[128,2048]{1,0:T(8,128)(2,1)S(1)} %collective-permute-done.9.refs_1_), channel_id=1, source_target_pairs={{0,16},{16,0},{32,48},{48,32},{64,80},{80,64},{96,112},{112,96},{1... | collective-permute-start | bytes 1572872 | tf_op jit(solution)/shard_map/ppermute | solution.py:24
  46.7 14.2 %collective-permute-start.14 = (bf16[128,2048]{1,0:T(8,128)(2,1)S(1)}, bf16[128,2048]{1,0:T(8,128)(2,1)S(1)}, u32[]{:S(2)}, u32[]{:S(2)}) collective-permute-start(bf16[128,2048]{1,0:T(8,128)(2,1)S(1)} %divide_convert_fusion.refs_1_), channel_id=1, source_target_pairs={{0,32},{16,48},{32,64},{48,80},{64,96},{80,112},{96,128},{112,144}... | collective-permute-start | bytes 1572872 | tf_op jit(solution)/shard_map/ppermute | solution.py:19
  46.9 14.0 %collective-permute-start.15 = (bf16[128,2048]{1,0:T(8,128)(2,1)S(1)}, bf16[128,2048]{1,0:T(8,128)(2,1)S(1)}, u32[]{:S(2)}, u32[]{:S(2)}) collective-permute-start(bf16[128,2048]{1,0:T(8,128)(2,1)S(1)} %divide_convert_fusion.1.refs_0_), channel_id=1, source_target_pairs={{0,224},{16,240},{32,0},{48,16},{64,32},{80,48},{96,64},{112,80},{... | collective-permute-start | bytes 1572872 | tf_op jit(solution)/shard_map/ppermute | solution.py:19
  60.9 4.1 %collective-permute-start.18 = (bf16[128,2048]{1,0:T(8,128)(2,1)S(1)}, bf16[128,2048]{1,0:T(8,128)(2,1)S(1)}, u32[]{:S(2)}, u32[]{:S(2)}) collective-permute-start(bf16[128,2048]{1,0:T(8,128)(2,1)S(1)} %collective-permute-done.14.refs_0_), channel_id=1, source_target_pairs={{0,16},{16,0},{32,48},{48,32},{64,80},{80,64},{96,112},{112,96},{1... | collective-permute-start | bytes 1572872 | tf_op jit(solution)/shard_map/ppermute | solution.py:24
  62.2 2.7 %collective-permute-start.19 = (bf16[128,2048]{1,0:T(8,128)(2,1)S(1)}, bf16[128,2048]{1,0:T(8,128)(2,1)S(1)}, u32[]{:S(2)}, u32[]{:S(2)}) collective-permute-start(bf16[128,2048]{1,0:T(8,128)(2,1)S(1)} %collective-permute-done.15.refs_1_), channel_id=1, source_target_pairs={{0,16},{16,0},{32,48},{48,32},{64,80},{80,64},{96,112},{112,96},{1... | collective-permute-start | bytes 1572872 | tf_op jit(solution)/shard_map/ppermute | solution.py:24
  62.2 14.2 %collective-permute-start.12 = (bf16[128,2048]{1,0:T(8,128)(2,1)S(1)}, bf16[128,2048]{1,0:T(8,128)(2,1)S(1)}, u32[]{:S(2)}, u32[]{:S(2)}) collective-permute-start(bf16[128,2048]{1,0:T(8,128)(2,1)S(1)} %collective-permute-done.8.refs_0_), channel_id=1, source_target_pairs={{0,32},{16,48},{32,64},{48,80},{64,96},{80,112},{96,128},{112,144}... | collective-permute-start | bytes 1572872 | tf_op jit(solution)/shard_map/ppermute | solution.py:19
  62.2 14.2 %collective-permute-start.13 = (bf16[128,2048]{1,0:T(8,128)(2,1)S(1)}, bf16[128,2048]{1,0:T(8,128)(2,1)S(1)}, u32[]{:S(2)}, u32[]{:S(2)}) collective-permute-start(bf16[128,2048]{1,0:T(8,128)(2,1)S(1)} %collective-permute-done.9.refs_1_), channel_id=1, source_target_pairs={{0,224},{16,240},{32,0},{48,16},{64,32},{80,48},{96,64},{112,80},{... | collective-permute-start | bytes 1572872 | tf_op jit(solution)/shard_map/ppermute | solution.py:19
  76.4 4.1 %collective-permute-start.24 = (bf16[128,2048]{1,0:T(8,128)(2,1)S(1)}, bf16[128,2048]{1,0:T(8,128)(2,1)S(1)}, u32[]{:S(2)}, u32[]{:S(2)}) collective-permute-start(bf16[128,2048]{1,0:T(8,128)(2,1)S(1)} %collective-permute-done.12.refs_0_), channel_id=1, source_target_pairs={{0,16},{16,0},{32,48},{48,32},{64,80},{80,64},{96,112},{112,96},{1... | collective-permute-start | bytes 1572872 | tf_op jit(solution)/shard_map/ppermute | solution.py:24
  77.8 2.7 %collective-permute-start.25 = (bf16[128,2048]{1,0:T(8,128)(2,1)S(1)}, bf16[128,2048]{1,0:T(8,128)(2,1)S(1)}, u32[]{:S(2)}, u32[]{:S(2)}) collective-permute-start(bf16[128,2048]{1,0:T(8,128)(2,1)S(1)} %collective-permute-done.13.refs_1_), channel_id=1, source_target_pairs={{0,16},{16,0},{32,48},{48,32},{64,80},{80,64},{96,112},{112,96},{1... | collective-permute-start | bytes 1572872 | tf_op jit(solution)/shard_map/ppermute | solution.py:24
  77.8 14.2 %collective-permute-start.22 = (bf16[128,2048]{1,0:T(8,128)(2,1)S(1)}, bf16[128,2048]{1,0:T(8,128)(2,1)S(1)}, u32[]{:S(2)}, u32[]{:S(2)}) collective-permute-start(bf16[128,2048]{1,0:T(8,128)(2,1)S(1)} %collective-permute-done.14.refs_0_), channel_id=1, source_target_pairs={{0,32},{16,48},{32,64},{48,80},{64,96},{80,112},{96,128},{112,144}... | collective-permute-start | bytes 1572872 | tf_op jit(solution)/shard_map/ppermute | solution.py:19
  80.2 12.7 %collective-permute-start.23 = (bf16[128,2048]{1,0:T(8,128)(2,1)S(1)}, bf16[128,2048]{1,0:T(8,128)(2,1)S(1)}, u32[]{:S(2)}, u32[]{:S(2)}) collective-permute-start(bf16[128,2048]{1,0:T(8,128)(2,1)S(1)} %collective-permute-done.15.refs_1_), channel_id=1, source_target_pairs={{0,224},{16,240},{32,0},{48,16},{64,32},{80,48},{96,64},{112,80},{... | collective-permute-start | bytes 1572872 | tf_op jit(solution)/shard_map/ppermute | solution.py:19
  92.9 4.6 %collective-permute-start.26 = (bf16[128,2048]{1,0:T(8,128)(2,1)S(1)}, bf16[128,2048]{1,0:T(8,128)(2,1)S(1)}, u32[]{:S(2)}, u32[]{:S(2)}) collective-permute-start(bf16[128,2048]{1,0:T(8,128)(2,1)S(1)} %collective-permute-done.22.refs_0_), channel_id=1, source_target_pairs={{0,16},{16,0},{32,48},{48,32},{64,80},{80,64},{96,112},{112,96},{1... | collective-permute-start | bytes 1572872 | tf_op jit(solution)/shard_map/ppermute | solution.py:24
  94.6 5.4 %collective-permute-start.27 = (bf16[128,2048]{1,0:T(8,128)(2,1)S(1)}, bf16[128,2048]{1,0:T(8,128)(2,1)S(1)}, u32[]{:S(2)}, u32[]{:S(2)}) collective-permute-start(bf16[128,2048]{1,0:T(8,128)(2,1)S(1)} %collective-permute-done.23.refs_1_), channel_id=1, source_target_pairs={{0,16},{16,0},{32,48},{48,32},{64,80},{80,64},{96,112},{112,96},{1... | collective-permute-start | bytes 1572872 | tf_op jit(solution)/shard_map/ppermute | solution.py:24
  94.6 14.2 %collective-permute-start.20 = (bf16[128,2048]{1,0:T(8,128)(2,1)S(1)}, bf16[128,2048]{1,0:T(8,128)(2,1)S(1)}, u32[]{:S(2)}, u32[]{:S(2)}) collective-permute-start(bf16[128,2048]{1,0:T(8,128)(2,1)S(1)} %collective-permute-done.12.refs_0_), channel_id=1, source_target_pairs={{0,32},{16,48},{32,64},{48,80},{64,96},{80,112},{96,128},{112,144}... | collective-permute-start | bytes 1572872 | tf_op jit(solution)/shard_map/ppermute | solution.py:19
  96.1 12.7 %collective-permute-start.21 = (bf16[128,2048]{1,0:T(8,128)(2,1)S(1)}, bf16[128,2048]{1,0:T(8,128)(2,1)S(1)}, u32[]{:S(2)}, u32[]{:S(2)}) collective-permute-start(bf16[128,2048]{1,0:T(8,128)(2,1)S(1)} %collective-permute-done.13.refs_1_), channel_id=1, source_target_pairs={{0,224},{16,240},{32,0},{48,16},{64,32},{80,48},{96,64},{112,80},{... | collective-permute-start | bytes 1572872 | tf_op jit(solution)/shard_map/ppermute | solution.py:19
  97.3 22.7 %collective-permute-start.34 = (bf16[128,2048]{1,0:T(8,128)(2,1)S(1)}, bf16[128,2048]{1,0:T(8,128)(2,1)S(1)}, u32[]{:S(2)}, u32[]{:S(2)}) collective-permute-start(bf16[128,2048]{1,0:T(8,128)(2,1)S(1)} %collective-permute-done.22.refs_0_), channel_id=1, source_target_pairs={{0,32},{16,48},{32,64},{48,80},{64,96},{80,112},{96,128},{112,144}... | collective-permute-start | bytes 1572872 | tf_op jit(solution)/shard_map/ppermute | solution.py:19
  97.5 22.7 %collective-permute-start.35 = (bf16[128,2048]{1,0:T(8,128)(2,1)S(1)}, bf16[128,2048]{1,0:T(8,128)(2,1)S(1)}, u32[]{:S(2)}, u32[]{:S(2)}) collective-permute-start(bf16[128,2048]{1,0:T(8,128)(2,1)S(1)} %collective-permute-done.23.refs_1_), channel_id=1, source_target_pairs={{0,224},{16,240},{32,0},{48,16},{64,32},{80,48},{96,64},{112,80},{... | collective-permute-start | bytes 1572872 | tf_op jit(solution)/shard_map/ppermute | solution.py:19
  108.8 14.1 %collective-permute-start.30 = (bf16[128,2048]{1,0:T(8,128)(2,1)S(1)}, bf16[128,2048]{1,0:T(8,128)(2,1)S(1)}, u32[]{:S(2)}, u32[]{:S(2)}) collective-permute-start(bf16[128,2048]{1,0:T(8,128)(2,1)S(1)} %collective-permute-done.20.refs_0_), channel_id=1, source_target_pairs={{0,16},{16,0},{32,48},{48,32},{64,80},{80,64},{96,112},{112,96},{1... | collective-permute-start | bytes 1572872 | tf_op jit(solution)/shard_map/ppermute | solution.py:24
  111.6 11.3 %collective-permute-start.31 = (bf16[128,2048]{1,0:T(8,128)(2,1)S(1)}, bf16[128,2048]{1,0:T(8,128)(2,1)S(1)}, u32[]{:S(2)}, u32[]{:S(2)}) collective-permute-start(bf16[128,2048]{1,0:T(8,128)(2,1)S(1)} %collective-permute-done.21.refs_1_), channel_id=1, source_target_pairs={{0,16},{16,0},{32,48},{48,32},{64,80},{80,64},{96,112},{112,96},{1... | collective-permute-start | bytes 1572872 | tf_op jit(solution)/shard_map/ppermute | solution.py:24
  111.6 19.6 %collective-permute-start.28 = (bf16[128,2048]{1,0:T(8,128)(2,1)S(1)}, bf16[128,2048]{1,0:T(8,128)(2,1)S(1)}, u32[]{:S(2)}, u32[]{:S(2)}) collective-permute-start(bf16[128,2048]{1,0:T(8,128)(2,1)S(1)} %collective-permute-done.20.refs_0_), channel_id=1, source_target_pairs={{0,32},{16,48},{32,64},{48,80},{64,96},{80,112},{96,128},{112,144}... | collective-permute-start | bytes 1572872 | tf_op jit(solution)/shard_map/ppermute | solution.py:19
  120.0 11.2 %collective-permute-start.29 = (bf16[128,2048]{1,0:T(8,128)(2,1)S(1)}, bf16[128,2048]{1,0:T(8,128)(2,1)S(1)}, u32[]{:S(2)}, u32[]{:S(2)}) collective-permute-start(bf16[128,2048]{1,0:T(8,128)(2,1)S(1)} %collective-permute-done.21.refs_1_), channel_id=1, source_target_pairs={{0,224},{16,240},{32,0},{48,16},{64,32},{80,48},{96,64},{112,80},{... | collective-permute-start | bytes 1572872 | tf_op jit(solution)/shard_map/ppermute | solution.py:19
  120.2 26.4 %collective-permute-start.36 = (bf16[128,2048]{1,0:T(8,128)(2,1)S(1)}, bf16[128,2048]{1,0:T(8,128)(2,1)S(1)}, u32[]{:S(2)}, u32[]{:S(2)}) collective-permute-start(bf16[128,2048]{1,0:T(8,128)(2,1)S(1)} %collective-permute-done.34.refs_0_), channel_id=1, source_target_pairs={{0,16},{16,0},{32,48},{48,32},{64,80},{80,64},{96,112},{112,96},{1... | collective-permute-start | bytes 1572872 | tf_op jit(solution)/shard_map/ppermute | solution.py:24
  122.8 23.8 %collective-permute-start.37 = (bf16[128,2048]{1,0:T(8,128)(2,1)S(1)}, bf16[128,2048]{1,0:T(8,128)(2,1)S(1)}, u32[]{:S(2)}, u32[]{:S(2)}) collective-permute-start(bf16[128,2048]{1,0:T(8,128)(2,1)S(1)} %collective-permute-done.35.refs_1_), channel_id=1, source_target_pairs={{0,16},{16,0},{32,48},{48,32},{64,80},{80,64},{96,112},{112,96},{1... | collective-permute-start | bytes 1572872 | tf_op jit(solution)/shard_map/ppermute | solution.py:24
  131.2 16.8 %collective-permute-start.32 = (bf16[128,2048]{1,0:T(8,128)(2,1)S(1)}, bf16[128,2048]{1,0:T(8,128)(2,1)}, u32[]{:S(2)}, u32[]{:S(2)}) collective-permute-start(bf16[128,2048]{1,0:T(8,128)(2,1)S(1)} %collective-permute-done.28.refs_0_), channel_id=1, source_target_pairs={{0,16},{16,0},{32,48},{48,32},{64,80},{80,64},{96,112},{112,96},{1... | collective-permute-start | bytes 1572872 | tf_op jit(solution)/shard_map/ppermute | solution.py:24
  134.3 13.7 %collective-permute-start.33 = (bf16[128,2048]{1,0:T(8,128)(2,1)S(1)}, bf16[128,2048]{1,0:T(8,128)(2,1)}, u32[]{:S(2)}, u32[]{:S(2)}) collective-permute-start(bf16[128,2048]{1,0:T(8,128)(2,1)S(1)} %collective-permute-done.29.refs_1_), channel_id=1, source_target_pairs={{0,16},{16,0},{32,48},{48,32},{64,80},{80,64},{96,112},{112,96},{1... | collective-permute-start | bytes 1572872 | tf_op jit(solution)/shard_map/ppermute | solution.py:24
  134.5 3.5 %collective-permute-start.38 = (bf16[16,32]{1,0:T(8,128)(2,1)S(1)}, bf16[16,32]{1,0:T(8,128)(2,1)S(1)}, u32[]{:S(2)}, u32[]{:S(2)}) collective-permute-start(bf16[16,32]{1,0:T(8,128)(2,1)S(1)} %reshape.21), channel_id=1, source_target_pairs={{4,0},{8,4},{12,8},{0,12},{5,1},{9,5},{13,9},{1,13},{6,2},{10,6},{... | collective-permute-start | bytes 3080 | tf_op jit(solution)/shard_map/ppermute | solution.py:139
  138.0 4.0 %collective-permute-start.39 = (bf16[16,32]{1,0:T(8,128)(2,1)S(1)}, bf16[16,32]{1,0:T(8,128)(2,1)S(1)}, u32[]{:S(2)}, u32[]{:S(2)}) collective-permute-start(bf16[16,32]{1,0:T(8,128)(2,1)S(1)} %reshape.21), channel_id=1, source_target_pairs={{8,0},{12,4},{0,8},{4,12},{9,1},{13,5},{1,9},{5,13},{10,2},{14,6},... | collective-permute-start | bytes 3080 | tf_op jit(solution)/shard_map/ppermute | solution.py:139
  142.0 3.9 %collective-permute-start.40 = (bf16[16,32]{1,0:T(8,128)(2,1)S(1)}, bf16[16,32]{1,0:T(8,128)(2,1)S(1)}, u32[]{:S(2)}, u32[]{:S(2)}) collective-permute-start(bf16[16,32]{1,0:T(8,128)(2,1)S(1)} %reshape.21), channel_id=1, source_target_pairs={{12,0},{0,4},{4,8},{8,12},{13,1},{1,5},{5,9},{9,13},{14,2},{2,6},{... | collective-permute-start | bytes 3080 | tf_op jit(solution)/shard_map/ppermute | solution.py:139
